TPU v7x, 32 devices: a whole 2x2x4 slice. The times are simulated.
32 devices in a mesh: row: 8 (over y, x, core), col: 4 (over z).
Axes of the slice: x: 2, y: 2, z: 4, core: 2. Of those that a mesh axis runs over, the one named last changes fastest.
Arguments:
- tokens: bfloat16 [256, 7168], P(('row', 'col')), may hold values from -6 to 6
- router_logits: float32 [256, 16], P(('row', 'col')), may hold values from -18 to 318
- expert_ids: int32 [256, 8], P(('row', 'col')), may hold values from 0 to 15, all different within a row; in each aligned block of 8 rows (0 to 7, 8 to 15, ...) at most 8 rows name the same one
- w_gate: bfloat16 [16, 7168, 2048], P('row', None, 'col'), may hold values from -0.3307189 to 0.3307189
- w_up: bfloat16 [16, 7168, 2048], P('row', None, 'col'), may hold values from -0.3307189 to 0.3307189
- w_down: bfloat16 [16, 2048, 7168], P('row', 'col'), may hold values from -0.61871843 to 0.61871843
Outputs:
- merged: bfloat16 [256, 7168], P(('row', 'col'))
Inputs may be any that keep to these rules, and one draw needn't show every extreme that they name: `expert_ids`: each row names 8 different experts. Among the 8 tokens of one device no expert is named more than 8 times, and in every draw some device names some expert exactly 8 times.
All inputs are finite; a program needn't handle non-finite values.
Results may differ from a plain program's by a relative error of at most 0.015.
Values may be sent and summed in bfloat16 or wider, within the bound.
A program may use at most 128 MiB of HBM per device.

v0:
```python
import jax
import jax.numpy as jnp
from jax import lax
from jax.sharding import PartitionSpec as P


def expert_rows(inputs, gate_weight, up_weight, down_weight):
    gate = jnp.einsum("...d,df->...f", inputs, gate_weight, preferred_element_type=jnp.float32)
    up = jnp.einsum("...d,df->...f", inputs, up_weight, preferred_element_type=jnp.float32)
    hidden = (jax.nn.silu(gate) * up).astype(jnp.bfloat16)
    return jnp.einsum("...f,fd->...d", hidden, down_weight, preferred_element_type=jnp.float32)


def local(tokens, router_logits, expert_ids, w_gate, w_up, w_down):
    groups = lax.axis_size("row")
    slices = lax.axis_size("col")
    per_group = w_gate.shape[0]
    experts = router_logits.shape[1]
    tok_count = tokens.shape[0]
    model_width = tokens.shape[1]
    picked = jnp.take_along_axis(router_logits, expert_ids, axis=1)
    probs = jax.nn.softmax(picked, axis=-1).astype(jnp.bfloat16)
    marks = expert_ids[:, :, None] == jnp.arange(experts, dtype=jnp.int32)[None, None, :]
    table = jnp.sum(probs.astype(jnp.float32)[:, :, None] * marks.astype(jnp.float32), axis=1)
    group_weight = table.astype(jnp.bfloat16).reshape(tok_count, groups, per_group)
    all_rows, all_weight = (
        lax.all_gather(tokens[None], ("row", "col"), axis=0, tiled=True),
        lax.all_gather(group_weight[None], ("row", "col"), axis=0, tiled=True),
    )
    all_rows = all_rows.reshape(groups, slices, tok_count, model_width)
    own_weight = lax.dynamic_index_in_dim(all_weight, lax.axis_index("row"), 2, keepdims=False)
    own_weight = own_weight.reshape(groups, slices, tok_count, per_group)
    weights = own_weight.astype(jnp.float32)
    total = jnp.zeros((groups, lax.axis_size("col") * 1, tok_count, model_width), jnp.float32)
    for inner in range(per_group):
        outputs = expert_rows(all_rows, w_gate[inner], w_up[inner], w_down[inner])
        total = total + outputs * weights[..., inner, None]
    sums = lax.psum_scatter(
        jnp.transpose(total, (1, 0, 2, 3)).astype(jnp.bfloat16),
        "col",
        scatter_dimension=0,
        tiled=True,
    )
    returned = lax.all_to_all(sums, "row", split_axis=1, concat_axis=1, tiled=True)
    return jnp.sum(returned[0].astype(jnp.float32), axis=0).astype(jnp.bfloat16)


def solution(mesh):
    in_specs = (
        P(("row", "col"), None),
        P(("row", "col"), None),
        P(("row", "col"), None),
        P("row", None, "col"),
        P("row", None, "col"),
        P("row", "col", None),
    )
    out_specs = P(("row", "col"), None)
    return jax.shard_map(local, mesh=mesh, in_specs=in_specs, out_specs=out_specs, check_vma=False)
```

profile of v0, /device:TPU:0, one launch (start us, length us, event | category | flops | bytes accessed | tf_op | source)
XLA Modules:
  0.0 284.5 jit_solution(13803126516886475972)
XLA Ops:
  6.5 0.0 copy-start
  6.5 0.0 all-gather.3.cloned.1.call-start
  6.5 0.7 all-gather.3.cloned.1.call-update
  7.3 0.0 all-reduce.3.cloned.1.call-start
  7.3 0.7 bitcast_or_fusion
  8.0 0.1 reshape.53
  8.1 0.0 copy-done
  8.1 0.7 gather_fusion
  8.8 0.1 reshape.56
  8.9 0.8 fusion.52
  9.7 0.9 fusion.48
  10.6 0.8 fusion.49
  11.4 0.8 select_reduce_fusion
  12.1 0.1 copy.16
  12.2 0.1 copy.17
  12.3 71.2 %all_gather.7 = bf16[32,8,8,2]{2,1,3,0:T(8,128)(2,1)S(1)} all-gather(bf16[1,8,8,2]{2,1,3,0:T(8,128)(2,1)S(1)} %copy.17), channel_id=1, replica_groups=mesh['row'=8,'col'=4] {'row','col'}, dimensions={0}, use_global_device_ids=true | all-gather | bytes 8448 | tf_op jit(solution)/shard_map/all_gather | solution.py:28
  83.5 0.1 constant_dynamic-slice_fusion.1
  83.6 0.5 copy.27
  84.1 0.0 all-gather.3.cloned.1.call-done
  84.1 0.0 copy-start.1
  84.1 0.0 copy-start.2
  84.1 6.4 %fusion.7 = f32[8,4,8,512]{3,2,1,0:T(8,128)S(1)} fusion(bf16[8,4,8,7168]{3,2,1,0:T(8,128)(2,1)} %bitcast.89, bf16[2,7168,512]{2,1,0:T(8,128)(2,1)} %param.9), kind=kOutput, calls=%fused_computation.10 | convolution fusion | flops 1879048192 | bytes 11534336 | tf_op jit(solution)/shard_map/...d,df->...f/dot_general | solution.py:8
  90.5 3.1 %copy-done.2 = bf16[2,7168,512]{2,1,0:T(8,128)(2,1)S(1)} copy-done((bf16[2,7168,512]{2,1,0:T(8,128)(2,1)S(1)}, bf16[2,7168,512]{2,1,0:T(8,128)(2,1)}, u32[]{:S(2)}) %copy-start.2) | copy-done | bytes 14680088
  93.6 2.0 fusion.12
  95.7 13.2 %fusion = f32[4,8,8,7168]{3,2,0,1:T(8,128)} fusion(bf16[2,512,7168]{2,1,0:T(8,128)(2,1)} %param.11, f32[4,8,8]{2,0,1:T(4,128)S(1)} %get-tuple-element.6, bf16[8,4,8,7168]{3,2,1,0:T(8,128)(2,1)} %bitcast.90, bf16[2,7168,512]{2,1,0:T(8,128)(2,1)} %param.10, f32[8,4,8,512]{3,2,1,0:T(8,128)S(1)} %fusion.7), kind=kOutput, calls=%fused_computation.2 | convolution fusion | flops 3760717824 | bytes 26215424 | tf_op jit(solution)/shard_map/...f,fd->...d/dot_general | solution.py:11
  108.9 13.9 %fusion.3 = bf16[4,8,8,7168]{3,2,0,1:T(8,128)(2,1)} fusion(f32[4,8,8,7168]{3,2,0,1:T(8,128)} %fusion, bf16[2,512,7168]{2,1,0:T(8,128)(2,1)} %param.11, f32[4,8,8]{2,0,1:T(4,128)S(1)} %get-tuple-element.5, bf16[8,4,8,7168]{3,2,1,0:T(8,128)(2,1)} %bitcast.91, bf16[2,7168,512]{2,1,0:T(8,128)(2,1)} %param.10, f32[8,4,8,512]{3,2,1,0:T(8,128)S(1)} %fusion.12), kind=kOutput, calls=%fused_computation.6 | convolution fusion | flops 3764387840 | bytes 29885440 | tf_op jit(solution)/shard_map/...f,fd->...d/dot_general | solution.py:11
  122.9 0.0 all-reduce.3.cloned.1.call-update
  122.9 0.6 dynamic-slice
  123.5 134.2 %all-reduce.3.cloned.1.call-done = bf16[4,8,8,7168]{3,2,0,1:T(8,128)(2,1)} async-done(((bf16[4,8,8,7168]{3,2,0,1:T(8,128)(2,1)}), bf16[4,8,8,7168]{3,2,0,1:T(8,128)(2,1)}) %all-reduce.3.cloned.1.call-update) | async-done | bytes 3670032
  257.7 1.9 constant_dynamic-slice_fusion
  259.5 17.4 %all_to_all.5 = bf16[1,8,8,7168]{3,2,0,1:T(8,128)(2,1)S(1)} all-to-all(bf16[1,8,8,7168]{3,2,0,1:T(8,128)(2,1)S(1)} %constant_dynamic-slice_fusion), channel_id=1, replica_groups=mesh['row'=8,'col'=4] {'row'}, dimensions={1} | all-to-all | bytes 1835008 | tf_op jit(solution)/shard_map/all_to_all | solution.py:44
  276.9 0.8 reduce_sum.32
  (5 shorter events, 0.0 us)
Async XLA Ops:
  6.5 1.6 copy-start
  6.5 77.6 %all-gather.3.cloned.1.call-start = ((), (), s32[]{:S(2)}) async-start(), calls=%async_computation.1 | async-start | bytes 3784704 | tf_op jit(solution)/shard_map/all_gather | solution.py:27
  7.3 250.4 %all-reduce.3.cloned.1.call-start = ((), (), s32[]{:S(2)}) async-start(), calls=%async_computation.2 | async-start | bytes 7340032
  84.1 6.4 %copy-start.1 = (bf16[256,7168]{1,0:T(8,128)(2,1)S(1)}, bf16[256,7168]{1,0:T(8,128)(2,1)}, u32[]{:S(2)}) copy-start(bf16[256,7168]{1,0:T(8,128)(2,1)} %all-gather.3.cloned.1.call-done) | copy-start | bytes 11010052
  84.1 9.5 %copy-start.2 = (bf16[2,7168,512]{2,1,0:T(8,128)(2,1)S(1)}, bf16[2,7168,512]{2,1,0:T(8,128)(2,1)}, u32[]{:S(2)}) copy-start(bf16[2,7168,512]{2,1,0:T(8,128)(2,1)} %param.9) | copy-start | bytes 44040196
  108.9 14.0 %copy-start.3 = (u32[32]{0:T(128)S(1)}, u32[32]{0:T(128)}, u32[]{:S(2)}) copy-start(u32[32]{0:T(128)} %constant.60) | copy-start | bytes 388
Sparse Core Ops, SparseCore 0:
  10.2 63.2 all-gather.2
  123.0 134.6 all-reduce.2
where the time goes:
time: 285 us
  waiting for transfers between devices  135 us (47%)
  blocking collectives  88.6 us (31%)
  matrix products  35.6 us (12%)
  between operations  13.5 us (5%)
  local copies, waits for them, and re-layouts  7.17 us (3%)
  other arithmetic  4.72 us (2%)
    unnamed x3, waiting for transfers between devices  135 us
    all_gather x1, blocking collectives, local(): lax.all_gather(group_weight[None], ('row', 'col'), axis=0, tiled=True)  71.2 us
    dot_general x2, matrix products, expert_rows(): jnp.einsum('...f,fd->...d', hidden, down_weight, preferred_element_type=j...  27.2 us
    all_to_all x1, blocking collectives, local(): lax.all_to_all(sums, 'row', split_axis=1, concat_axis=1, tiled=True)  17.4 us
    dot_general x2, matrix products, expert_rows(): jnp.einsum('...d,df->...f', inputs, gate_weight, preferred_element_type=j...  8.43 us
    unnamed x11, local copies, waits for them, and re-layouts  6 us
  transfers between devices with their start and end apart: 2, of which 1 were waited for; matrix products, arithmetic and copies ran while one was open for 2% of the time, Pallas kernels for 0%

commit v1 on v0

v1 whole, which is shorter than its diff:
```python
import functools
import jax
import jax.numpy as jnp
from jax import lax
from jax.experimental import pallas as pl
from jax.experimental.pallas import tpu as pltpu
from jax.sharding import PartitionSpec as P

MESH = pl.DeviceIdType.MESH
LANES = 128


def column_chunks(width, wanted):
    tiles = width // LANES
    count = max(n for n in range(1, wanted + 1) if tiles % n == 0)
    return count, width // count


def split_parts(width, count):
    tiles = width // LANES
    edges = [tiles * i // count * LANES for i in range(count + 1)]
    return [(edges[i], edges[i + 1] - edges[i]) for i in range(count)]


class Copies:
    def __init__(self, send_sems, recv_sems):
        self.send_sems, self.recv_sems, self.used, self.sent = send_sems, recv_sems, 0, []

    def start(self, src, dst, target):
        n = self.used
        self.used += 1
        copy = pltpu.make_async_remote_copy(
            src_ref=src,
            dst_ref=dst,
            send_sem=self.send_sems.at[n],
            recv_sem=self.recv_sems.at[n],
            device_id=target,
            device_id_type=MESH,
        )
        copy.start()
        self.sent.append(copy)
        return copy


def kernel(
    n_row, n_col, count, chunk,
    tokens_hbm, logits_hbm, ids_hbm, gate_hbm, up_hbm, down_hbm,
    out_ref,
    tok, logits, ids, table_own, wg, wu, wd,
    zbuf, ztab, xbuf, xtab, acc, hid, part, rcore, rstage, p3, r4,
    small_sems, weight_sems, send_sems, recv_sems,
):
    bits = n_row.bit_length() - 1
    upper = list(range(1, bits))
    tok_count = tok.shape[0]
    rows = n_col * tok_count
    per_group, ff = wg.shape[1], wg.shape[3]
    total = n_row * rows
    experts = logits.shape[1]

    row, col = lax.axis_index("row"), lax.axis_index("col")
    mine = [(row // 2**i) % 2 for i in range(bits)]

    def across(i):
        return {"row": row + 2**i * (1 - 2 * mine[i]), "col": col}

    def along(j):
        return {"row": row, "col": (col + j) % n_col}

    def at(fixed, *tail):
        return tuple(fixed.get(i, slice(None)) for i in reversed(range(bits))) + (slice(None),) + tail

    orders = [upper[p:] + upper[:p] for p in range(len(upper))]

    small = [
        pltpu.make_async_copy(src, dst, small_sems.at[i])
        for i, (src, dst) in enumerate(((tokens_hbm, tok), (logits_hbm, logits), (ids_hbm, ids)))
    ]
    for copy in small:
        copy.start()
    gate_up, down = [], []
    for c in range(count):
        span = pl.ds(c * chunk, chunk)
        pair = [
            pltpu.make_async_copy(gate_hbm.at[:, span, :], wg.at[c], weight_sems.at[0, c]),
            pltpu.make_async_copy(up_hbm.at[:, span, :], wu.at[c], weight_sems.at[1, c]),
        ]
        for copy in pair:
            copy.start()
        gate_up.append(pair)
    for c in range(count):
        copy = pltpu.make_async_copy(down_hbm.at[:, :, pl.ds(c * chunk, chunk)], wd.at[c], weight_sems.at[2, c])
        copy.start()
        down.append(copy)

    barrier = pltpu.get_barrier_semaphore()
    peers = [across(i) for i in range(bits)] + [along(j) for j in range(1, n_col)]
    for peer in peers:
        pl.semaphore_signal(barrier, inc=1, device_id=peer, device_id_type=MESH)

    small[1].wait()
    small[2].wait()
    scores, named = logits[...], ids[...]
    lane = lax.broadcasted_iota(jnp.int32, scores.shape, 1)
    marks = jnp.zeros(scores.shape, jnp.float32)
    for k in range(named.shape[1]):
        marks = marks + jnp.where(named[:, k : k + 1] == lane, 1.0, 0.0)
    chosen = marks > 0.5
    top = jnp.max(jnp.where(chosen, scores, -jnp.inf), axis=1, keepdims=True)
    weight = jnp.where(chosen, jnp.exp(jnp.where(chosen, scores, top) - top), 0.0)
    weight = weight / jnp.sum(weight, axis=1, keepdims=True)
    table_own[...] = jnp.zeros(table_own.shape, table_own.dtype)
    table_own[:, :experts] = weight.astype(table_own.dtype)
    small[0].wait()

    pl.semaphore_wait(barrier, len(peers))
    copies = Copies(send_sems, recv_sems)

    parts = split_parts(chunk, len(upper))
    pieces = [(table_own, ztab, xtab, [(0, LANES)])]
    pieces += [(tok.at[:, pl.ds(c * chunk, chunk)], zbuf.at[c], xbuf.at[c], parts) for c in range(count)]
    flights = []
    for own, z, _, _ in pieces:
        flights.append([copies.start(own, z.at[col], along(j)) for j in range(1, n_col)])
        z[col] = own[...]

    def gather_first(n):
        own, z, x, spans = pieces[n]
        for copy in flights[n]:
            copy.wait_recv()
        block = z[...].astype(jnp.float32).reshape(rows, z.shape[-1]).astype(x.dtype)
        x[at({i: mine[i] for i in range(bits)}, slice(None))] = block
        gather_stage(n, 0)

    def gather_stage(n, k):
        _, _, x, spans = pieces[n]
        flights[n] = []
        for p, (offset, width) in enumerate(spans):
            done = orders[p][:k]
            fixed = {i: mine[i] for i in range(bits) if i not in done}
            view = x.at[at(fixed, pl.ds(offset, width))]
            flights[n].append(copies.start(view, view, across(orders[p][k])))

    def gather_next(n, k):
        for copy in flights[n]:
            copy.wait_recv()
        if k < len(upper):
            gather_stage(n, k)
        else:
            _, _, x, _ = pieces[n]
            view = x.at[at({0: mine[0]}, slice(None))]
            flights[n] = [copies.start(view, view, across(0))]

    def gate_and_up(c):
        for copy in flights[c + 1]:
            copy.wait_recv()
        for copy in gate_up[c]:
            copy.wait()

        @pl.loop(0, per_group)
        def _(e):
            x = xbuf[c].reshape(total, chunk)
            for i, w in enumerate((wg, wu)):
                product = jnp.dot(x, w[c, e], preferred_element_type=jnp.float32)
                if c == 0:
                    acc[e, i] = product
                else:
                    acc[e, i] += product

    stages = len(upper) + 2
    for t in range(count + stages - 1):
        for k in range(stages):
            c = t - k
            if not 0 <= c < count:
                continue
            for n in ((0, 1) if c == 0 else (c + 1,)):
                if k == 0:
                    gather_first(n)
                elif k < stages - 1:
                    gather_next(n, k)
            if k == stages - 1:
                gate_and_up(c)

    for copy in flights[0]:
        copy.wait_recv()
    table = xtab[...].reshape(total, LANES).astype(jnp.float32)
    lane = lax.broadcasted_iota(jnp.int32, table.shape, 1)
    for e in range(per_group):
        weight = jnp.sum(jnp.where(lane == row * per_group + e, table, 0.0), axis=1, keepdims=True)
        gate, up = acc[e, 0], acc[e, 1]
        hidden = gate / (1.0 + jnp.exp(-gate)) * up * weight
        hid[:, e * ff : (e + 1) * ff] = hidden.astype(hid.dtype)

    tile = max(w for w in (LANES, 2 * LANES) if chunk % w == 0)
    spread = (2,) * bits
    returns = [None] * count

    def project(c):
        down[c].wait()

        @pl.loop(0, chunk // tile)
        def _(i):
            span = pl.ds(pl.multiple_of(i * tile, tile), tile)
            w = wd[c, :, :, span].reshape(per_group * ff, tile)
            product = jnp.dot(hid[...], w, preferred_element_type=jnp.float32)
            part[(c,) + (slice(None),) * (bits + 1) + (span,)] = (
                product.astype(part.dtype).reshape(spread + (rows, tile))
            )

        view = part.at[c].at[at({0: 1 - mine[0]}, slice(None))]
        returns[c] = [copies.start(view, rcore.at[c], across(0))]

    def reduce_stage(c, k):
        for copy in returns[c]:
            copy.wait_recv()
        chunk_part = part.at[c]
        if k == 0:
            index = at({0: mine[0]}, slice(None))
            both = chunk_part[index].astype(jnp.float32) + rcore[c].astype(jnp.float32)
            chunk_part[index] = both.astype(part.dtype)
        else:
            for p, (offset, width) in enumerate(parts):
                fixed = {i: mine[i] for i in [0] + orders[p][:k]}
                index = at(fixed, pl.ds(offset, width))
                both = chunk_part[index].astype(jnp.float32) + arrived(c, k - 1, p)[...].astype(jnp.float32)
                if k < len(upper):
                    chunk_part[index] = both.astype(part.dtype)
                else:
                    p3[c, :, :, offset : offset + width] = (
                        both.reshape(n_col, tok_count, width).astype(p3.dtype)
                    )
        returns[c] = []
        if k < len(upper):
            for p, (offset, width) in enumerate(parts):
                fixed = {i: mine[i] for i in [0] + orders[p][:k]}
                fixed[orders[p][k]] = 1 - mine[orders[p][k]]
                view = chunk_part.at[at(fixed, pl.ds(offset, width))]
                returns[c].append(copies.start(view, arrived(c, k, p), across(orders[p][k])))
        else:
            for j in range(1, n_col):
                returns[c].append(copies.start(p3.at[c, (col + j) % n_col], r4.at[c, j - 1], along(j)))

    def arrived(c, k, p):
        offset, width = parts[p]
        free = len(upper) - 1 - k
        return rstage[k].at[(c,) + (slice(None),) * (free + 1) + (pl.ds(offset, width),)]

    def finish(c):
        for copy in returns[c]:
            copy.wait_recv()
        whole = p3[c, col].astype(jnp.float32)
        for j in range(1, n_col):
            whole = whole + r4[c, j - 1].astype(jnp.float32)
        out_ref[:, c * chunk : (c + 1) * chunk] = whole.astype(out_ref.dtype)

    last = len(upper) + 2
    for t in range(count + last):
        for k in range(last + 1):
            c = t - k
            if not 0 <= c < count:
                continue
            if k == 0:
                project(c)
            elif k < last:
                reduce_stage(c, k - 1)
            else:
                finish(c)

    for copy in copies.sent:
        copy.wait_send()


def local(n_row, n_col, tokens, router_logits, expert_ids, w_gate, w_up, w_down):
    tok_count, width = tokens.shape
    per_group, _, ff = w_gate.shape
    rows = n_col * tok_count
    bits = n_row.bit_length() - 1
    count, chunk = column_chunks(width, CHUNKS)
    spread = (2,) * bits
    b16, f32 = jnp.bfloat16, jnp.float32
    upper = bits - 1
    sends = (n_col - 1) + upper + 1 + count * 2 * ((n_col - 1) + upper * upper + 1)
    scratch = [
        pltpu.VMEM(tokens.shape, b16),
        pltpu.VMEM(router_logits.shape, f32),
        pltpu.VMEM(expert_ids.shape, jnp.int32),
        pltpu.VMEM((tok_count, LANES), b16),
        pltpu.VMEM((count, per_group, chunk, ff), b16),
        pltpu.VMEM((count, per_group, chunk, ff), b16),
        pltpu.VMEM((count, per_group, ff, chunk), b16),
        pltpu.VMEM((count, n_col, tok_count, chunk), b16),
        pltpu.VMEM((n_col, tok_count, LANES), b16),
        pltpu.VMEM((count,) + spread + (rows, chunk), b16),
        pltpu.VMEM(spread + (rows, LANES), b16),
        pltpu.VMEM((per_group, 2, n_row * rows, ff), f32),
        pltpu.VMEM((n_row * rows, per_group * ff), b16),
        pltpu.VMEM((count,) + spread + (rows, chunk), b16),
        pltpu.VMEM((count,) + spread[1:] + (rows, chunk), b16),
        [pltpu.VMEM((count,) + (2,) * (upper - 1 - k) + (rows, chunk), b16) for k in range(upper)],
        pltpu.VMEM((count, n_col, tok_count, chunk), b16),
        pltpu.VMEM((count, n_col - 1, tok_count, chunk), b16),
        pltpu.SemaphoreType.DMA((3,)),
        pltpu.SemaphoreType.DMA((3, count)),
        pltpu.SemaphoreType.DMA((sends,)),
        pltpu.SemaphoreType.DMA((sends,)),
    ]
    return pl.pallas_call(
        functools.partial(kernel, n_row, n_col, count, chunk),
        out_shape=jax.ShapeDtypeStruct(tokens.shape, b16),
        in_specs=[pl.BlockSpec(memory_space=pl.ANY)] * 6,
        out_specs=pl.BlockSpec(memory_space=pltpu.VMEM),
        scratch_shapes=scratch,
        compiler_params=pltpu.CompilerParams(
            collective_id=0, has_side_effects=True, vmem_limit_bytes=67043328
        ),
    )(tokens, router_logits, expert_ids, w_gate, w_up, w_down)


CHUNKS = 4


def solution(mesh):
    in_specs = (
        P(("row", "col"), None),
        P(("row", "col"), None),
        P(("row", "col"), None),
        P("row", None, "col"),
        P("row", None, "col"),
        P("row", "col", None),
    )
    body = functools.partial(local, mesh.shape["row"], mesh.shape["col"])
    return jax.shard_map(
        body, mesh=mesh, in_specs=in_specs, out_specs=P(("row", "col"), None), check_vma=False
    )
```

time: 285 us -> 76 us (0.27)
  waiting for transfers between devices: 135 us -> 0 us
  blocking collectives: 88.6 us -> 0 us
  Pallas kernels: 0 us -> 74.3 us
  matrix products: 35.6 us -> 0 us
  between operations: 13.5 us -> 0.01 us
  local copies, waits for them, and re-layouts: 7.17 us -> 1.55 us
  other arithmetic: 4.72 us -> 0 us
    unnamed x3 -> x0, waiting for transfers between devices: 135 us -> none
    pallas_call x0 -> x1, Pallas kernels: none -> 74.3 us  [local(): pl.pallas_call(functools.partial(kernel, n_row, n_col, count, chunk), out...]
    all_gather x1 -> x0, blocking collectives: 71.2 us -> none  [local(): lax.all_gather(group_weight[None], ('row', 'col'), axis=0, tiled=True)]
    dot_general x4 -> x0, matrix products: 35.6 us -> none  [the longest x2 27.2 us: expert_rows(): jnp.einsum('...f,fd->...d', hidden, down_weight, preferred_element_type=j...]
    all_to_all x1 -> x0, blocking collectives: 17.4 us -> none  [local(): lax.all_to_all(sums, 'row', split_axis=1, concat_axis=1, tiled=True)]
    unnamed x11 -> x1, local copies, waits for them, and re-layouts: 6 us -> 1.55 us
  transfers between devices with their start and end apart: 2 -> 0, of which waited for: 1 -> 0; matrix products, arithmetic and copies ran while one was open for 2% -> 0% of each run, Pallas kernels for 0% -> 0%
where the time goes in v1:
time: 76 us; the launch traced here: 75.8 us
  Pallas kernels  74.3 us (98%)
  local copies, waits for them, and re-layouts  1.55 us (2%)
    pallas_call x1, Pallas kernels, local(): pl.pallas_call(functools.partial(kernel, n_row, n_col, count, chunk), out...  74.3 us
    unnamed x1, local copies, waits for them, and re-layouts  1.55 us

profile of v1, /device:TPU:0, one launch (start us, length us, event | category | flops | bytes accessed | tf_op | source)
XLA Modules:
  0.0 75.8 jit_solution(16000335403631240559)
XLA Ops:
  0.0 74.3 %shard_map.64 = bf16[8,7168]{1,0:T(8,128)(2,1)} custom-call(bf16[8,7168]{1,0:T(8,128)(2,1)} %tokens_hbm.1, f32[8,16]{1,0:T(8,128)} %logits_hbm.1, s32[8,8]{1,0:T(8,128)} %ids_hbm.1, bf16[2,7168,512]{2,1,0:T(8,128)(2,1)} %gate_hbm.1, bf16[2,7168,512]{2,1,0:T(8,128)(2,1)} %up_hbm.1, bf16[2,512,7168]{2,1,0:T(8,128)(2,1)} %down_hbm.1), custom_call_target="tpu_custom_call" | custom-call | tf_op jit(solution)/shard_map/pallas_call | solution.py:307
  74.3 1.6 %copy.8 = bf16[8,7168]{1,0:T(8,128)(2,1)} copy(bf16[8,7168]{1,0:T(8,128)(2,1)} %shard_map.64) | data formatting | bytes 229376

commit v2 on v1

--- a/solution.py
+++ b/solution.py
@@ -20,6 +20,12 @@
     tiles = width // LANES
     edges = [tiles * i // count * LANES for i in range(count + 1)]
     return [(edges[i], edges[i + 1] - edges[i]) for i in range(count)]
+
+
+def plan(count, lags, stages):
+    step = (lags[-1] - lags[0]) / (len(lags) - 1)
+    lags = list(lags) + [lags[-1] + step * (i + 1) for i in range(stages - len(lags))]
+    return sorted(((c, k) for c in range(count) for k in range(stages)), key=lambda e: (e[0] + lags[e[1]], e[1]))
 
 
 class Copies:
@@ -85,18 +91,43 @@
             pltpu.make_async_copy(gate_hbm.at[:, span, :], wg.at[c], weight_sems.at[0, c]),
             pltpu.make_async_copy(up_hbm.at[:, span, :], wu.at[c], weight_sems.at[1, c]),
         ]
-        for copy in pair:
-            copy.start()
         gate_up.append(pair)
     for c in range(count):
         copy = pltpu.make_async_copy(down_hbm.at[:, :, pl.ds(c * chunk, chunk)], wd.at[c], weight_sems.at[2, c])
-        copy.start()
         down.append(copy)
 
     barrier = pltpu.get_barrier_semaphore()
     peers = [across(i) for i in range(bits)] + [along(j) for j in range(1, n_col)]
     for peer in peers:
         pl.semaphore_signal(barrier, inc=1, device_id=peer, device_id_type=MESH)
+
+    small[0].wait()
+
+    pl.semaphore_wait(barrier, len(peers))
+    copies = Copies(send_sems, recv_sems)
+
+    parts = split_parts(chunk, len(upper))
+    pieces = [(table_own, ztab, xtab, [(0, LANES)])]
+    pieces += [(tok.at[:, pl.ds(c * chunk, chunk)], zbuf.at[c], xbuf.at[c], parts) for c in range(count)]
+    flights = [None] * len(pieces)
+
+    def send_own(n):
+        own, z, _, _ = pieces[n]
+        flights[n] = [copies.start(own, z.at[col], along(j)) for j in range(1, n_col)]
+        z[col] = own[...]
+
+    def start_all(started):
+        for copy in started:
+            copy.start()
+
+    stages = len(upper) + 2
+    events = plan(count, GATHER_LAGS, stages + 3)
+    ahead = next(i for i, e in enumerate(events) if e[1] == 3)
+    for c, k in events[:ahead]:
+        if k == 0:
+            send_own(c + 1)
+        else:
+            start_all(gate_up[c] if k == 1 else [down[c]])
 
     small[1].wait()
     small[2].wait()
@@ -111,18 +142,7 @@
     weight = weight / jnp.sum(weight, axis=1, keepdims=True)
     table_own[...] = jnp.zeros(table_own.shape, table_own.dtype)
     table_own[:, :experts] = weight.astype(table_own.dtype)
-    small[0].wait()
-
-    pl.semaphore_wait(barrier, len(peers))
-    copies = Copies(send_sems, recv_sems)
-
-    parts = split_parts(chunk, len(upper))
-    pieces = [(table_own, ztab, xtab, [(0, LANES)])]
-    pieces += [(tok.at[:, pl.ds(c * chunk, chunk)], zbuf.at[c], xbuf.at[c], parts) for c in range(count)]
-    flights = []
-    for own, z, _, _ in pieces:
-        flights.append([copies.start(own, z.at[col], along(j)) for j in range(1, n_col)])
-        z[col] = own[...]
+    send_own(0)
 
     def gather_first(n):
         own, z, x, spans = pieces[n]
@@ -167,19 +187,21 @@
                 else:
                     acc[e, i] += product
 
-    stages = len(upper) + 2
-    for t in range(count + stages - 1):
-        for k in range(stages):
-            c = t - k
-            if not 0 <= c < count:
-                continue
-            for n in ((0, 1) if c == 0 else (c + 1,)):
-                if k == 0:
-                    gather_first(n)
-                elif k < stages - 1:
-                    gather_next(n, k)
-            if k == stages - 1:
-                gate_and_up(c)
+    for c, k in events[ahead:]:
+        if k == 0:
+            send_own(c + 1)
+            continue
+        if k in (1, 2):
+            start_all(gate_up[c] if k == 1 else [down[c]])
+            continue
+        k -= 3
+        for n in (0, c + 1) if c == count // 2 else (c + 1,):
+            if k == 0:
+                gather_first(n)
+            elif k < stages - 1:
+                gather_next(n, k)
+        if k == stages - 1:
+            gate_and_up(c)
 
     for copy in flights[0]:
         copy.wait_recv()
@@ -254,17 +276,13 @@
         out_ref[:, c * chunk : (c + 1) * chunk] = whole.astype(out_ref.dtype)
 
     last = len(upper) + 2
-    for t in range(count + last):
-        for k in range(last + 1):
-            c = t - k
-            if not 0 <= c < count:
-                continue
-            if k == 0:
-                project(c)
-            elif k < last:
-                reduce_stage(c, k - 1)
-            else:
-                finish(c)
+    for c, k in plan(count, RETURN_LAGS, last + 1):
+        if k == 0:
+            project(c)
+        elif k < last:
+            reduce_stage(c, k - 1)
+        else:
+            finish(c)
 
     for copy in copies.sent:
         copy.wait_send()
@@ -317,6 +335,8 @@
 
 
 CHUNKS = 4
+GATHER_LAGS = (-1.5, -1.2, 1.8, 0, 1, 2, 3)
+RETURN_LAGS = (0, 1, 2, 3, 4)
 
 
 def solution(mesh):

time: 76 us -> 64.4 us (0.85)
  Pallas kernels: 74.3 us -> 62.6 us
    pallas_call x1, Pallas kernels: 74.3 us -> 62.6 us  [local(): pl.pallas_call(functools.partial(kernel, n_row, n_col, count, chunk), out...]
where the time goes in v2:
time: 64.4 us; the launch traced here: 64.2 us
  Pallas kernels  62.6 us (97%)
  local copies, waits for them, and re-layouts  1.55 us (2%)
    pallas_call x1, Pallas kernels, local(): pl.pallas_call(functools.partial(kernel, n_row, n_col, count, chunk), out...  62.6 us
    unnamed x1, local copies, waits for them, and re-layouts  1.55 us

profile of v2, /device:TPU:0, one launch (start us, length us, event | category | flops | bytes accessed | tf_op | source)
XLA Modules:
  0.0 64.2 jit_solution(2704869410439413536)
XLA Ops:
  0.0 62.6 %shard_map.64 = bf16[8,7168]{1,0:T(8,128)(2,1)} custom-call(bf16[8,7168]{1,0:T(8,128)(2,1)} %tokens_hbm.1, f32[8,16]{1,0:T(8,128)} %logits_hbm.1, s32[8,8]{1,0:T(8,128)} %ids_hbm.1, bf16[2,7168,512]{2,1,0:T(8,128)(2,1)} %gate_hbm.1, bf16[2,7168,512]{2,1,0:T(8,128)(2,1)} %up_hbm.1, bf16[2,512,7168]{2,1,0:T(8,128)(2,1)} %down_hbm.1), custom_call_target="tpu_custom_call" | custom-call | tf_op jit(solution)/shard_map/pallas_call | solution.py:325
  62.7 1.6 %copy.8 = bf16[8,7168]{1,0:T(8,128)(2,1)} copy(bf16[8,7168]{1,0:T(8,128)(2,1)} %shard_map.64) | data formatting | bytes 229376
